TPU v7x, 32 devices: a whole 2x2x4 slice. The times are simulated.
32 devices in a mesh: pair: 4 (over y, x), aux: 8 (over z, core).
Axes of the slice: x: 2, y: 2, z: 4, core: 2. Of those that a mesh axis runs over, the one named last changes fastest.
Arguments:
- same_panels: bfloat16 [32, 2, 112, 59904], P('aux', None, None, 'pair'), may hold values from -1 to 1
- opposite_panels: bfloat16 [32, 2, 112, 59904], P('aux', None, None, 'pair'), may hold values from -1 to 1
- same_amplitudes: bfloat16 [32, 112, 112], replicated, may hold values from -2 to 2
- opposite_amplitudes: bfloat16 [32, 112, 112], replicated, may hold values from -2 to 2
- same_energies: float32 [32, 2, 112], replicated, may hold values from 0.5 to 3
- opposite_energies: float32 [32, 2, 112], replicated, may hold values from 0.5 to 3
- same_ranks: int32 [32], replicated, may hold values from 48 to 112
- opposite_ranks: int32 [32], replicated, may hold values from 48 to 112
Outputs:
- same_residual: float32 [32, 112, 112], P('pair', 'aux')
- opposite_residual: float32 [32, 112, 112], P('pair', 'aux')
Inputs may be any that keep to these rules, and one draw needn't show every extreme that they name: `same_ranks`: slots at or beyond a pair's rank are padding. `opposite_ranks`: slots at or beyond a pair's rank are padding.
All inputs are finite; a program needn't handle non-finite values.
Results may differ from a plain program's by a relative error of at most 0.0013.
Values may be sent and summed in bfloat16 or wider, within the bound.
No kernel may reach another device: no remote copies, remote signals or barrier semaphores. Data moves between devices by JAX's collectives and lax.ppermute only.
A program may use at most 128 MiB of HBM per device.

v0:
```python
import jax
import jax.numpy as jnp
from jax import lax
from jax.sharding import PartitionSpec as P


def slot_mask(ranks, slots):
    places = jnp.arange(slots, dtype=jnp.int32)
    return (places[None, :] < ranks[:, None]).astype(jnp.float32)


def masked_amplitudes(amplitudes, keep):
    outer = keep[:, :, None] * keep[:, None, :]
    return (amplitudes.astype(jnp.float32) * outer).astype(jnp.bfloat16)


def dressing_total(panels, masked):
    mixed = jnp.einsum("pab,pbn->pan", masked, panels[:, 1], preferred_element_type=jnp.float32)
    return jnp.sum(panels[:, 0].astype(jnp.float32) * mixed, axis=(0, 1))


def partial_terms(panels, coupling):
    exchange = jnp.einsum(
        "pan,pbn->pab", panels[:, 0], panels[:, 1], preferred_element_type=jnp.float32
    )
    scaled = (panels[:, 0].astype(jnp.float32) * coupling[None, None, :]).astype(jnp.bfloat16)
    coulomb = jnp.einsum("pan,pbn->pab", scaled, panels[:, 1], preferred_element_type=jnp.float32)
    return exchange + coulomb


def finish_rows(summed, amplitudes, energies, ranks, pair_start, row_start):
    count = summed.shape[0]
    rows = summed.shape[1]
    slots = amplitudes.shape[1]
    keep = slot_mask(lax.dynamic_slice_in_dim(ranks, pair_start, count, 0), slots)
    amplitude = lax.dynamic_slice_in_dim(amplitudes, pair_start, count, 0)
    masked = masked_amplitudes(amplitude, keep)
    masked_rows = lax.dynamic_slice_in_dim(masked, row_start, rows, 1).astype(jnp.float32)
    energy = lax.dynamic_slice_in_dim(energies, pair_start, count, 0)
    first_gap = lax.dynamic_slice_in_dim(energy[:, 0], row_start, rows, 1)
    keep_rows = lax.dynamic_slice_in_dim(keep, row_start, rows, 1)
    diagonal = (first_gap[:, :, None] + energy[:, 1][:, None, :]) * masked_rows
    return (summed + diagonal) * (keep_rows[:, :, None] * keep[:, None, :])


def local_masked(amplitudes, ranks, start, count):
    slots = amplitudes.shape[1]
    keep = slot_mask(lax.dynamic_slice_in_dim(ranks, start, count, 0), slots)
    return masked_amplitudes(lax.dynamic_slice_in_dim(amplitudes, start, count, 0), keep)


def body(
    same_panels,
    opposite_panels,
    same_amplitudes,
    opposite_amplitudes,
    same_energies,
    opposite_energies,
    same_ranks,
    opposite_ranks,
):
    block_count = same_panels.shape[0]
    pair_index = lax.axis_index("pair")
    aux_index = lax.axis_index("aux")
    owned = block_count * lax.axis_size("aux") // lax.axis_size("pair")
    rows = same_amplitudes.shape[1] // lax.axis_size("aux")
    start = aux_index * block_count
    same_masked = local_masked(same_amplitudes, same_ranks, start, block_count)
    opposite_masked = local_masked(opposite_amplitudes, opposite_ranks, start, block_count)
    partial_coupling = dressing_total(same_panels, same_masked) + dressing_total(
        opposite_panels, opposite_masked
    )
    coupling = lax.psum(partial_coupling, "aux")
    same_rows, opposite_rows = (
        lax.all_to_all(
            partial_terms(same_panels, coupling), "aux", split_axis=1, concat_axis=0, tiled=True
        ),
        lax.all_to_all(
            partial_terms(opposite_panels, coupling), "aux", split_axis=1, concat_axis=0, tiled=True
        ),
    )
    same_sum, opposite_sum = (
        lax.psum_scatter(same_rows, "pair", scatter_dimension=0, tiled=True),
        lax.psum_scatter(opposite_rows, "pair", scatter_dimension=0, tiled=True),
    )
    pair_start = pair_index * owned
    row_start = aux_index * rows
    same_residual = finish_rows(
        same_sum, same_amplitudes, same_energies, same_ranks, pair_start, row_start
    )
    opposite_residual = finish_rows(
        opposite_sum, opposite_amplitudes, opposite_energies, opposite_ranks, pair_start, row_start
    )
    return (same_residual, opposite_residual)


def solution(mesh):
    placed = (
        P("aux", None, None, "pair"),
        P("aux", None, None, "pair"),
        P(),
        P(),
        P(),
        P(),
        P(),
        P(),
    )
    return jax.shard_map(
        body,
        mesh=mesh,
        in_specs=placed,
        out_specs=(P("pair", "aux", None), P("pair", "aux", None)),
        check_vma=False,
    )
```

profile of v0, /device:TPU:0, one launch (start us, length us, event | category | flops | bytes accessed | tf_op | source)
XLA Modules:
  0.0 178.4 jit_solution(11435442703354790816)
XLA Ops:
  7.2 0.7 dynamic_slice.49
  7.9 0.1 fusion.52
  8.0 0.7 dynamic_slice.51
  8.7 0.1 fusion.53
  8.8 10.7 %fusion = f32[14976]{0:T(1024)S(1)} fusion(bf16[4,2,112,14976]{3,2,1,0:T(8,128)(2,1)} %param.8, f32[4,112]{1,0:T(4,128)S(1)} %fusion.52, bf16[32,112,112]{2,1,0:T(8,128)(2,1)} %param.10, s32[]{:T(128)S(6)} %select_n.6), kind=kOutput, calls=%fused_computation.4 | convolution fusion | flops 1523185024 | bytes 27015684 | tf_op jit(solution)/shard_map/pab,pbn->pan/dot_general | solution.py:18
  19.5 10.8 %fusion.2 = f32[14976]{0:T(1024)S(1)} fusion(bf16[4,2,112,14976]{3,2,1,0:T(8,128)(2,1)} %param.9, f32[4,112]{1,0:T(4,128)S(1)} %fusion.53, bf16[32,112,112]{2,1,0:T(8,128)(2,1)} %param.11, s32[]{:T(128)S(6)} %select_n.6), kind=kOutput, calls=%fused_computation.6 | convolution fusion | flops 1523185024 | bytes 27015684 | tf_op jit(solution)/shard_map/pab,pbn->pan/dot_general | solution.py:18
  30.3 30.8 %psum.7 = f32[14976]{0:T(1024)S(1)} all-reduce(f32[14976]{0:T(1024)S(1)} %add.78), channel_id=1, replica_groups=mesh['pair'=4,'aux'=8] {'aux'}, use_global_device_ids=true, to_apply=%region_2.0 | all-reduce | flops 14976 | bytes 119808 | tf_op jit(solution)/shard_map/psum | solution.py:73
  61.1 10.6 %fusion.6 = f32[4,112,112]{2,1,0:T(8,128)S(1)} fusion(f32[14976]{0:T(1024)S(1)} %psum.7, bf16[4,2,112,14976]{3,2,1,0:T(8,128)(2,1)} %param.8), kind=kOutput, calls=%fused_computation.9 | convolution fusion | flops 1522999296 | bytes 27097600 | tf_op jit(solution)/shard_map/pan,pbn->pab/dot_general | solution.py:27
  71.7 10.6 %fusion.32 = f32[4,112,112]{2,1,0:T(8,128)S(1)} fusion(f32[4,112,112]{2,1,0:T(8,128)S(1)} %fusion.6, bf16[4,2,112,14976]{3,2,1,0:T(8,128)(2,1)} %param.8), kind=kOutput, calls=%fused_computation.34 | convolution fusion | flops 1502921728 | bytes 27238400 | tf_op jit(solution)/shard_map/pan,pbn->pab/dot_general | solution.py:23
  82.3 0.0 copy-start
  82.3 0.8 copy.64
  83.1 3.6 %all-to-all-start = ((f32[4,112,112]{2,0,1:T(4,128)}), f32[4,112,112]{2,0,1:T(4,128)S(1)}, u32[]{:S(2)}, u32[]{:S(2)}) async-start(f32[4,112,112]{2,0,1:T(4,128)} %copy.64), calls=%async_computation | async-start | bytes 458752 | tf_op jit(solution)/shard_map/all_to_all | solution.py:75
  86.7 10.6 %fusion.4 = f32[4,112,112]{2,1,0:T(8,128)S(1)} fusion(f32[14976]{0:T(1024)S(1)} %psum.7, bf16[4,2,112,14976]{3,2,1,0:T(8,128)(2,1)} %param.9), kind=kOutput, calls=%fused_computation.8 | convolution fusion | flops 1522999296 | bytes 27097600 | tf_op jit(solution)/shard_map/pan,pbn->pab/dot_general | solution.py:27
  97.3 0.0 copy-start.1
  97.3 0.0 copy-done
  97.3 0.1 dynamic_slice.55
  97.4 0.1 fusion.48
  97.5 10.6 %fusion.37 = f32[4,112,112]{2,1,0:T(8,128)S(1)} fusion(f32[4,112,112]{2,1,0:T(8,128)S(1)} %fusion.4, bf16[4,2,112,14976]{3,2,1,0:T(8,128)(2,1)} %param.9), kind=kOutput, calls=%fused_computation.35 | convolution fusion | flops 1502921728 | bytes 27238400 | tf_op jit(solution)/shard_map/pan,pbn->pab/dot_general | solution.py:23
  108.1 0.1 constant_dynamic-slice_fusion.7
  108.2 0.7 constant_dynamic-slice_fusion.11
  108.9 0.0 copy-done.1
  108.9 0.1 dynamic_slice.61
  109.0 0.8 copy.71
  109.7 0.8 constant_dynamic-slice_fusion.5
  110.5 0.1 fusion.49
  110.6 0.0 all-to-all-done
  110.6 4.8 %all-to-all-start.1 = ((f32[4,112,112]{2,0,1:T(4,128)}), f32[4,112,112]{2,0,1:T(4,128)S(1)}, u32[]{:S(2)}, u32[]{:S(2)}) async-start(f32[4,112,112]{2,0,1:T(4,128)} %copy.71), calls=%async_computation.2 | async-start | bytes 458752 | tf_op jit(solution)/shard_map/all_to_all | solution.py:78
  115.4 0.0 reduce-scatter.3.cloned.1.call-start
  115.5 0.7 copy.65
  116.2 0.0 reduce-scatter.3.cloned.1.call-update
  116.2 0.0 reduce-scatter.5.cloned.1.call-start
  116.3 0.1 constant_dynamic-slice_fusion.2
  116.4 0.1 copy.76
  116.5 0.1 copy.69
  116.6 0.1 copy.70
  116.6 0.1 copy.67
  116.7 0.1 copy.77
  116.8 0.1 copy.74
  116.9 1.0 constant_dynamic-slice_fusion.4
  117.9 1.0 constant_dynamic-slice_fusion.9
  118.8 5.6 %all-to-all-done.1 = f32[4,112,112]{2,0,1:T(4,128)S(1)} async-done(((f32[4,112,112]{2,0,1:T(4,128)}), f32[4,112,112]{2,0,1:T(4,128)S(1)}, u32[]{:S(2)}, u32[]{:S(2)}) %all-to-all-start.1) | async-done | bytes 200736 | tf_op jit(solution)/shard_map/all_to_all | solution.py:78
  124.4 0.7 copy.72
  125.2 0.0 reduce-scatter.5.cloned.1.call-update
  125.2 0.7 constant_dynamic-slice_fusion.6
  125.9 17.9 %reduce-scatter.3.cloned.1.call-done = f32[8,14,112]{2,0,1:T(8,128)} async-done(((f32[32,14,112]{2,0,1:T(8,128)}), f32[8,14,112]{2,0,1:T(8,128)}) %reduce-scatter.3.cloned.1.call-update) | async-done | bytes 50192 | tf_op jit(solution)/shard_map/reduce_scatter | solution.py:83
  143.9 1.6 multiply_multiply_fusion.1
  145.4 24.6 %reduce-scatter.5.cloned.1.call-done = f32[8,14,112]{2,0,1:T(8,128)} async-done(((f32[32,14,112]{2,0,1:T(8,128)}), f32[8,14,112]{2,0,1:T(8,128)}) %reduce-scatter.5.cloned.1.call-update) | async-done | bytes 50192 | tf_op jit(solution)/shard_map/reduce_scatter | solution.py:84
  170.1 1.6 multiply_multiply_fusion
  (3 shorter events, 0.0 us)
Async XLA Ops:
  82.3 15.0 %copy-start = (s32[32]{0:T(128)S(1)}, s32[32]{0:T(128)}, u32[]{:S(2)}) copy-start(s32[32]{0:T(128)} %param.14) | copy-start | bytes 388
  83.1 27.5 %all-to-all-start = ((f32[4,112,112]{2,0,1:T(4,128)}), f32[4,112,112]{2,0,1:T(4,128)S(1)}, u32[]{:S(2)}, u32[]{:S(2)}) async-start(f32[4,112,112]{2,0,1:T(4,128)} %copy.64), calls=%async_computation | async-start | bytes 458752 | tf_op jit(solution)/shard_map/all_to_all | solution.py:75
  97.3 11.6 %copy-start.1 = (s32[32]{0:T(128)S(1)}, s32[32]{0:T(128)}, u32[]{:S(2)}) copy-start(s32[32]{0:T(128)} %param.15) | copy-start | bytes 388
  110.6 13.8 %all-to-all-start.1 = ((f32[4,112,112]{2,0,1:T(4,128)}), f32[4,112,112]{2,0,1:T(4,128)S(1)}, u32[]{:S(2)}, u32[]{:S(2)}) async-start(f32[4,112,112]{2,0,1:T(4,128)} %copy.71), calls=%async_computation.2 | async-start | bytes 458752 | tf_op jit(solution)/shard_map/all_to_all | solution.py:78
  115.4 28.4 %reduce-scatter.3.cloned.1.call-start = ((), (), s32[]{:S(2)}) async-start(), calls=%async_computation.4 | async-start | bytes 286720 | tf_op jit(solution)/shard_map/reduce_scatter | solution.py:83
  116.2 53.8 %reduce-scatter.5.cloned.1.call-start = ((), (), s32[]{:S(2)}) async-start(), calls=%async_computation.5 | async-start | bytes 286720 | tf_op jit(solution)/shard_map/reduce_scatter | solution.py:84
Sparse Core Ops, SparseCore 0:
  119.0 24.7 reduce-scatter.2
  146.7 23.3 reduce-scatter.4
where the time goes:
time: 179 us; the launch traced here: 178 us
  matrix products  63.9 us (36%)
  waiting for transfers between devices  48.2 us (27%)
  blocking collectives  30.8 us (17%)
  between operations  14.2 us (8%)
  local copies, waits for them, and re-layouts  9.48 us (5%)
  starting transfers between devices  8.49 us (5%)
  other arithmetic  3.41 us (2%)
    psum x1, blocking collectives, body(): coupling = lax.psum(partial_coupling, 'aux')  30.8 us
    reduce_scatter x1, waiting for transfers between devices, body(): lax.psum_scatter(opposite_rows, 'pair', scatter_dimension=0, tiled=True)  24.6 us
    dot_general x2, matrix products, dressing_total(): jnp.einsum('pab,pbn->pan', masked, panels[:, 1], preferred_element_type=j...  21.5 us
    dot_general x2, matrix products, partial_terms(): jnp.einsum('pan,pbn->pab', panels[:, 0], panels[:, 1], preferred_element_...  21.2 us
    dot_general x2, matrix products, partial_terms(): jnp.einsum('pan,pbn->pab', scaled, panels[:, 1], preferred_element_type=j...  21.2 us
    reduce_scatter x1, waiting for transfers between devices, body(): lax.psum_scatter(same_rows, 'pair', scatter_dimension=0, tiled=True)  17.9 us
    all_to_all x1, waiting for transfers between devices, body(): lax.all_to_all(partial_terms(opposite_panels, coupling), 'aux', split_axi...  5.62 us
    all_to_all x1, starting transfers between devices, body(): lax.all_to_all(partial_terms(opposite_panels, coupling), 'aux', split_axi...  4.83 us
  transfers between devices with their start and end apart: 4, of which 3 were waited for; matrix products, arithmetic and copies ran while one was open for 17% of the time, Pallas kernels for 0%

commit v1 on v0

--- a/solution.py
+++ b/solution.py
@@ -70,7 +70,7 @@
     partial_coupling = dressing_total(same_panels, same_masked) + dressing_total(
         opposite_panels, opposite_masked
     )
-    coupling = lax.psum(partial_coupling, "aux")
+    coupling = jnp.sum(lax.all_gather(partial_coupling, "aux"), axis=0)
     same_rows, opposite_rows = (
         lax.all_to_all(
             partial_terms(same_panels, coupling), "aux", split_axis=1, concat_axis=0, tiled=True

time: 179 us -> 167 us (0.933)
  blocking collectives: 30.8 us -> 16.5 us
    psum x1 -> x0, blocking collectives: 30.8 us -> none  [body(): coupling = lax.psum(partial_coupling, 'aux')]
    all_gather x0 -> x1, blocking collectives: none -> 16.5 us  [body(): coupling = jnp.sum(lax.all_gather(partial_coupling, 'aux'), axis=0)]
  transfers between devices with their start and end apart: 4 -> 4, of which waited for: 3 -> 3; matrix products, arithmetic and copies ran while one was open for 17% -> 18% of each run, Pallas kernels for 0% -> 0%
where the time goes in v1:
time: 167 us; the launch traced here: 166 us
  matrix products  63.9 us (38%)
  waiting for transfers between devices  48.2 us (29%)
  blocking collectives  16.5 us (10%)
  between operations  14.2 us (9%)
  starting transfers between devices  9.86 us (6%)
  local copies, waits for them, and re-layouts  9.53 us (6%)
  other arithmetic  3.76 us (2%)
    reduce_scatter x1, waiting for transfers between devices, body(): lax.psum_scatter(opposite_rows, 'pair', scatter_dimension=0, tiled=True)  24.6 us
    dot_general x2, matrix products, dressing_total(): jnp.einsum('pab,pbn->pan', masked, panels[:, 1], preferred_element_type=j...  21.5 us
    dot_general x2, matrix products, partial_terms(): jnp.einsum('pan,pbn->pab', scaled, panels[:, 1], preferred_element_type=j...  21.2 us
    dot_general x2, matrix products, partial_terms(): jnp.einsum('pan,pbn->pab', panels[:, 0], panels[:, 1], preferred_element_...  21.2 us
    reduce_scatter x1, waiting for transfers between devices, body(): lax.psum_scatter(same_rows, 'pair', scatter_dimension=0, tiled=True)  17.9 us
    all_gather x1, blocking collectives, body(): coupling = jnp.sum(lax.all_gather(partial_coupling, 'aux'), axis=0)  16.5 us
    all_to_all x1, waiting for transfers between devices, body(): lax.all_to_all(partial_terms(opposite_panels, coupling), 'aux', split_axi...  5.62 us
    all_to_all x1, starting transfers between devices, body(): lax.all_to_all(partial_terms(opposite_panels, coupling), 'aux', split_axi...  5.08 us
  transfers between devices with their start and end apart: 4, of which 3 were waited for; matrix products, arithmetic and copies ran while one was open for 18% of the time, Pallas kernels for 0%

profile of v1, /device:TPU:0, one launch (start us, length us, event | category | flops | bytes accessed | tf_op | source)
XLA Modules:
  0.0 165.9 jit_solution(9484555093031298861)
XLA Ops:
  7.2 0.7 dynamic_slice.49
  7.9 0.1 fusion.52
  8.0 0.7 dynamic_slice.51
  8.7 0.1 fusion.53
  8.8 10.7 %fusion = f32[14976]{0:T(1024)S(1)} fusion(bf16[4,2,112,14976]{3,2,1,0:T(8,128)(2,1)} %param.8, f32[4,112]{1,0:T(4,128)S(1)} %fusion.52, bf16[32,112,112]{2,1,0:T(8,128)(2,1)} %param.10, s32[]{:T(128)S(6)} %select_n.6), kind=kOutput, calls=%fused_computation.4 | convolution fusion | flops 1523185024 | bytes 27015684 | tf_op jit(solution)/shard_map/pab,pbn->pan/dot_general | solution.py:18
  19.5 10.8 %fusion.2 = f32[14976]{0:T(1024)S(1)} fusion(bf16[4,2,112,14976]{3,2,1,0:T(8,128)(2,1)} %param.9, f32[4,112]{1,0:T(4,128)S(1)} %fusion.53, bf16[32,112,112]{2,1,0:T(8,128)(2,1)} %param.11, s32[]{:T(128)S(6)} %select_n.6), kind=kOutput, calls=%fused_computation.6 | convolution fusion | flops 1523185024 | bytes 27015684 | tf_op jit(solution)/shard_map/pab,pbn->pan/dot_general | solution.py:18
  30.4 16.5 %all-gather.1 = f32[8,1,14976]{2,1,0:T(1,128)S(1)} all-gather(f32[1,1,14976]{2,1,0:T(1,128)S(1)} %reshape.178), channel_id=2, replica_groups=mesh['pair'=4,'aux'=8] {'aux'}, dimensions={0}, use_global_device_ids=true | all-gather | bytes 539136 | tf_op jit(solution)/shard_map/all_gather | solution.py:73
  46.8 0.4 reduce_sum.29
  47.2 10.6 %fusion.6 = f32[4,112,112]{2,1,0:T(8,128)S(1)} fusion(f32[14976]{0:T(1024)S(1)} %reduce_sum.29, bf16[4,2,112,14976]{3,2,1,0:T(8,128)(2,1)} %param.8), kind=kOutput, calls=%fused_computation.9 | convolution fusion | flops 1522999296 | bytes 27097600 | tf_op jit(solution)/shard_map/pan,pbn->pab/dot_general | solution.py:27
  57.8 10.6 %fusion.32 = f32[4,112,112]{2,1,0:T(8,128)S(1)} fusion(f32[4,112,112]{2,1,0:T(8,128)S(1)} %fusion.6, bf16[4,2,112,14976]{3,2,1,0:T(8,128)(2,1)} %param.8), kind=kOutput, calls=%fused_computation.34 | convolution fusion | flops 1502921728 | bytes 27238400 | tf_op jit(solution)/shard_map/pan,pbn->pab/dot_general | solution.py:23
  68.4 0.0 copy-start
  68.4 0.8 copy.64
  69.2 4.7 %all-to-all-start = ((f32[4,112,112]{2,0,1:T(4,128)}), f32[4,112,112]{2,0,1:T(4,128)S(1)}, u32[]{:S(2)}, u32[]{:S(2)}) async-start(f32[4,112,112]{2,0,1:T(4,128)} %copy.64), calls=%async_computation | async-start | bytes 458752 | tf_op jit(solution)/shard_map/all_to_all | solution.py:75
  73.9 10.6 %fusion.4 = f32[4,112,112]{2,1,0:T(8,128)S(1)} fusion(f32[14976]{0:T(1024)S(1)} %reduce_sum.29, bf16[4,2,112,14976]{3,2,1,0:T(8,128)(2,1)} %param.9), kind=kOutput, calls=%fused_computation.8 | convolution fusion | flops 1522999296 | bytes 27097600 | tf_op jit(solution)/shard_map/pan,pbn->pab/dot_general | solution.py:27
  84.5 0.0 copy-start.1
  84.5 0.0 copy-done
  84.5 0.1 dynamic_slice.55
  84.6 0.1 fusion.48
  84.7 10.6 %fusion.37 = f32[4,112,112]{2,1,0:T(8,128)S(1)} fusion(f32[4,112,112]{2,1,0:T(8,128)S(1)} %fusion.4, bf16[4,2,112,14976]{3,2,1,0:T(8,128)(2,1)} %param.9), kind=kOutput, calls=%fused_computation.35 | convolution fusion | flops 1502921728 | bytes 27238400 | tf_op jit(solution)/shard_map/pan,pbn->pab/dot_general | solution.py:23
  95.3 0.1 constant_dynamic-slice_fusion.7
  95.4 0.7 constant_dynamic-slice_fusion.11
  96.1 0.0 copy-done.1
  96.1 0.1 dynamic_slice.61
  96.1 0.8 copy.71
  96.9 0.8 constant_dynamic-slice_fusion.5
  97.7 0.1 fusion.49
  97.8 0.0 all-to-all-done
  97.8 5.1 %all-to-all-start.1 = ((f32[4,112,112]{2,0,1:T(4,128)}), f32[4,112,112]{2,0,1:T(4,128)S(1)}, u32[]{:S(2)}, u32[]{:S(2)}) async-start(f32[4,112,112]{2,0,1:T(4,128)} %copy.71), calls=%async_computation.2 | async-start | bytes 458752 | tf_op jit(solution)/shard_map/all_to_all | solution.py:78
  102.9 0.0 reduce-scatter.3.cloned.1.call-start
  102.9 0.7 copy.65
  103.7 0.0 reduce-scatter.3.cloned.1.call-update
  103.7 0.0 reduce-scatter.5.cloned.1.call-start
  103.7 0.1 constant_dynamic-slice_fusion.2
  103.8 0.1 copy.76
  103.9 0.1 copy.69
  104.0 0.1 copy.70
  104.1 0.1 copy.67
  104.2 0.1 copy.77
  104.2 0.1 copy.74
  104.3 1.0 constant_dynamic-slice_fusion.4
  105.3 1.0 constant_dynamic-slice_fusion.9
  106.3 5.6 %all-to-all-done.1 = f32[4,112,112]{2,0,1:T(4,128)S(1)} async-done(((f32[4,112,112]{2,0,1:T(4,128)}), f32[4,112,112]{2,0,1:T(4,128)S(1)}, u32[]{:S(2)}, u32[]{:S(2)}) %all-to-all-start.1) | async-done | bytes 200736 | tf_op jit(solution)/shard_map/all_to_all | solution.py:78
  111.9 0.7 copy.72
  112.6 0.0 reduce-scatter.5.cloned.1.call-update
  112.7 0.7 constant_dynamic-slice_fusion.6
  113.4 17.9 %reduce-scatter.3.cloned.1.call-done = f32[8,14,112]{2,0,1:T(8,128)} async-done(((f32[32,14,112]{2,0,1:T(8,128)}), f32[8,14,112]{2,0,1:T(8,128)}) %reduce-scatter.3.cloned.1.call-update) | async-done | bytes 50192 | tf_op jit(solution)/shard_map/reduce_scatter | solution.py:83
  131.3 1.6 multiply_multiply_fusion.1
  132.9 24.6 %reduce-scatter.5.cloned.1.call-done = f32[8,14,112]{2,0,1:T(8,128)} async-done(((f32[32,14,112]{2,0,1:T(8,128)}), f32[8,14,112]{2,0,1:T(8,128)}) %reduce-scatter.5.cloned.1.call-update) | async-done | bytes 50192 | tf_op jit(solution)/shard_map/reduce_scatter | solution.py:84
  157.5 1.6 multiply_multiply_fusion
  (4 shorter events, 0.1 us)
Async XLA Ops:
  68.4 16.1 %copy-start = (s32[32]{0:T(128)S(1)}, s32[32]{0:T(128)}, u32[]{:S(2)}) copy-start(s32[32]{0:T(128)} %param.14) | copy-start | bytes 388
  69.2 28.6 %all-to-all-start = ((f32[4,112,112]{2,0,1:T(4,128)}), f32[4,112,112]{2,0,1:T(4,128)S(1)}, u32[]{:S(2)}, u32[]{:S(2)}) async-start(f32[4,112,112]{2,0,1:T(4,128)} %copy.64), calls=%async_computation | async-start | bytes 458752 | tf_op jit(solution)/shard_map/all_to_all | solution.py:75
  84.5 11.6 %copy-start.1 = (s32[32]{0:T(128)S(1)}, s32[32]{0:T(128)}, u32[]{:S(2)}) copy-start(s32[32]{0:T(128)} %param.15) | copy-start | bytes 388
  97.8 14.1 %all-to-all-start.1 = ((f32[4,112,112]{2,0,1:T(4,128)}), f32[4,112,112]{2,0,1:T(4,128)S(1)}, u32[]{:S(2)}, u32[]{:S(2)}) async-start(f32[4,112,112]{2,0,1:T(4,128)} %copy.71), calls=%async_computation.2 | async-start | bytes 458752 | tf_op jit(solution)/shard_map/all_to_all | solution.py:78
  102.9 28.5 %reduce-scatter.3.cloned.1.call-start = ((), (), s32[]{:S(2)}) async-start(), calls=%async_computation.4 | async-start | bytes 286720 | tf_op jit(solution)/shard_map/reduce_scatter | solution.py:83
  103.7 53.8 %reduce-scatter.5.cloned.1.call-start = ((), (), s32[]{:S(2)}) async-start(), calls=%async_computation.5 | async-start | bytes 286720 | tf_op jit(solution)/shard_map/reduce_scatter | solution.py:84
Sparse Core Ops, SparseCore 0:
  106.5 24.8 reduce-scatter.2
  134.1 23.3 reduce-scatter.4
